TPU v7x, 32 devices: a whole 2x2x4 slice. The times are simulated.
32 devices in a mesh: cp: 8 (over z, x), tp: 4 (over y, core).
Axes of the slice: x: 2, y: 2, z: 4, core: 2. Of those that a mesh axis runs over, the one named last changes fastest.
Arguments:
- queries: bfloat16 [1536, 2048], P('cp', 'tp'), may hold values from -128 to 128
- keys: bfloat16 [1536, 256], P('cp'), may hold values from -6 to 6
- values: bfloat16 [1536, 256], P('cp'), may hold values from -6 to 6
- positions: int32 [1536], replicated, may hold values from 0 to 1535, as said below
- out_weight: bfloat16 [2048, 8192], P('tp'), may hold values from -0.125 to 0.125
Outputs:
- mixed: bfloat16 [1536, 8192], P(('cp', 'tp'))
Inputs may be any that keep to these rules, and one draw needn't show every extreme that they name: positions is a permutation of 0 to 1535. The tokens stored at indices d * 192 to (d + 1) * 192 - 1 form two runs of 96 consecutive positions, the first starting at b * 96 and the second at (15 - b) * 96 for some b, each b used by one d.
All inputs are finite; a program needn't handle non-finite values.
Results may differ from a plain program's by a relative error of at most 0.013.
Values may be sent and summed in bfloat16 or wider, within the bound.
A program may use at most 128 MiB of HBM per device.

v0:
```python
import jax
import jax.numpy as jnp
from jax import lax
from jax.sharding import PartitionSpec as P

HEAD = 128
GROUP = 8


def shards(queries, keys, values, positions, out_weight):
    tok_rows = queries.shape[0]
    head_count = queries.shape[1] // HEAD
    score_scale = HEAD ** (-0.5)
    kv_group = lax.axis_index("tp") * head_count // GROUP
    own_keys = lax.dynamic_slice_in_dim(keys, kv_group * HEAD, HEAD, 1)
    own_values = lax.dynamic_slice_in_dim(values, kv_group * HEAD, HEAD, 1)
    query_pos = lax.dynamic_slice_in_dim(positions, lax.axis_index("cp") * tok_rows, tok_rows, 0)
    local_queries = queries.reshape(tok_rows, head_count, HEAD)
    run_max = jnp.full((tok_rows, head_count), -1e30, jnp.float32)
    arrived_keys = lax.all_gather(own_keys, "cp", axis=0, tiled=True)
    arrived_values = lax.all_gather(own_values, "cp", axis=0, tiled=True)
    allowed = (positions[None, :] <= query_pos[:, None])[:, None, :]
    scores = (
        jnp.einsum("qhd,kd->qhk", local_queries, arrived_keys, preferred_element_type=jnp.float32)
        * score_scale
    )
    scores = jnp.where(allowed, scores, -1e30)
    new_max = jnp.maximum(run_max, jnp.max(scores, axis=-1))
    weights = jnp.where(allowed, jnp.exp(scores - new_max[:, :, None]), 0.0)
    run_sum = jnp.sum(weights, axis=-1)
    run_out = jnp.einsum(
        "qhk,kd->qhd",
        weights.astype(jnp.bfloat16),
        arrived_values,
        preferred_element_type=jnp.float32,
    )
    final_state = (new_max, run_sum, run_out)
    run_max, run_sum, run_out = final_state
    attended = (
        (run_out / run_sum[:, :, None]).astype(jnp.bfloat16).reshape(tok_rows, head_count * HEAD)
    )
    return lax.psum_scatter(
        jnp.dot(attended, out_weight, preferred_element_type=jnp.float32).astype(jnp.bfloat16),
        "tp",
        scatter_dimension=0,
        tiled=True,
    )


def solution(mesh):
    in_specs = (P("cp", "tp"), P("cp", None), P("cp", None), P(), P("tp", None))
    out_specs = P(("cp", "tp"), None)
    return jax.shard_map(shards, mesh=mesh, in_specs=in_specs, out_specs=out_specs, check_vma=False)
```

profile of v0, /device:TPU:0, one launch (start us, length us, event | category | flops | bytes accessed | tf_op | source)
XLA Modules:
  0.0 127.3 jit_solution(13655687156293303523)
XLA Ops:
  6.5 0.0 copy-start
  6.5 0.0 copy-start.1
  6.5 0.0 reduce-scatter.2.cloned.1.call-start
  6.5 0.8 constant_dynamic-slice_fusion.1
  7.4 32.8 %all_gather.6 = bf16[1536,128]{1,0:T(8,128)(2,1)S(1)} all-gather(bf16[192,128]{1,0:T(8,128)(2,1)S(1)} %constant_dynamic-slice_fusion.1), channel_id=1, replica_groups=mesh['cp'=8,'tp'=4] {'cp'}, dimensions={0}, use_global_device_ids=true | all-gather | bytes 442368 | tf_op jit(solution)/shard_map/all_gather | solution.py:20
  40.2 0.8 dynamic_slice.9
  40.9 0.9 broadcast_compare_fusion
  41.9 0.0 copy-done
  41.9 1.1 fusion
  43.0 0.0 copy-done.1
  43.0 31.0 %all_gather.7 = bf16[1536,128]{1,0:T(8,128)(2,1)S(1)} all-gather(bf16[192,128]{1,0:T(8,128)(2,1)S(1)} %constant_dynamic-slice_fusion), channel_id=1, replica_groups=mesh['cp'=8,'tp'=4] {'cp'}, dimensions={0}, use_global_device_ids=true | all-gather | bytes 442368 | tf_op jit(solution)/shard_map/all_gather | solution.py:21
  74.0 0.0 slice-start
  74.0 1.5 %fusion.1 = f32[192,4]{0,1:T(4,128)S(1)} fusion(f32[1536,192,4]{0,1,2:T(8,128)S(1)} %get-tuple-element.6, f32[192,4]{0,1:T(4,128)S(1)} %broadcast_maximum_fusion, pred[192,1536]{1,0:T(8,128)(4,1)S(1)} %broadcast_compare_fusion), kind=kLoop, calls=%fused_computation.4 | loop fusion | flops 5897472 | bytes 5019648 | tf_op jit(solution)/shard_map/reduce_sum | solution.py:30
  75.5 0.0 slice-start.1
  75.5 1.4 %fusion.12 = bf16[4,24,8,128]{3,2,1,0:T(8,128)(2,1)S(1)} fusion(f32[1536,192,4]{0,1,2:T(8,128)S(1)} %get-tuple-element.6, f32[192,4]{0,1:T(4,128)S(1)} %broadcast_maximum_fusion, pred[192,1536]{1,0:T(8,128)(4,1)S(1)} %broadcast_compare_fusion, bf16[1536,128]{1,0:T(8,128)(2,1)S(1)} %all_gather.7, f32[192,4]{0,1:T(4,128)S(1)} %fusion.1), kind=kOutput, calls=%fused_computation.10 | convolution fusion | flops 308084736 | bytes 5609472 | tf_op jit(solution)/shard_map/qhk,kd->qhd/dot_general | solution.py:31
  76.9 0.0 slice-done
  76.9 0.9 slice-done.1
  77.8 3.5 %convolution_convert_fusion = bf16[192,8192]{1,0:T(8,128)(2,1)} fusion(bf16[512,8192]{1,0:T(8,128)(2,1)S(1)} %bitcast.41, bf16[4,24,8,128]{3,2,1,0:T(8,128)(2,1)S(1)} %fusion.12), kind=kOutput, calls=%fused_computation | convolution fusion | flops 1612185600 | bytes 11730944 | tf_op jit(solution)/shard_map/dot_general | solution.py:43
  81.3 0.0 reduce-scatter.2.cloned.1.call-update
  81.3 39.2 %reduce-scatter.2.cloned.1.call-done = bf16[48,8192]{1,0:T(8,128)(2,1)} async-done(((bf16[192,8192]{1,0:T(8,128)(2,1)}), bf16[48,8192]{1,0:T(8,128)(2,1)}) %reduce-scatter.2.cloned.1.call-update) | async-done | bytes 786448 | tf_op jit(solution)/shard_map/reduce_scatter | solution.py:42
  (3 shorter events, 0.0 us)
Async XLA Ops:
  6.5 35.3 %copy-start = (bf16[192,512]{1,0:T(8,128)(2,1)S(1)}, bf16[192,512]{1,0:T(8,128)(2,1)}, u32[]{:S(2)}) copy-start(bf16[192,512]{1,0:T(8,128)(2,1)} %param.5) | copy-start | bytes 589828
  6.5 36.4 %copy-start.1 = (bf16[192,256]{1,0:T(8,128)(2,1)S(1)}, bf16[192,256]{1,0:T(8,128)(2,1)}, u32[]{:S(2)}) copy-start(bf16[192,256]{1,0:T(8,128)(2,1)} %param.7) | copy-start | bytes 294916
  6.5 114.0 %reduce-scatter.2.cloned.1.call-start = ((), (), s32[]{:S(2)}) async-start(), calls=%async_computation.1 | async-start | bytes 3932160 | tf_op jit(solution)/shard_map/reduce_scatter | solution.py:42
  74.0 2.9 %slice-start = ((s8[8388608]{0:T(1024)(128)(4,1)}), s8[4194304]{0:T(1024)(128)(4,1)S(1)}, s32[]{:S(2)}) async-start(s8[8388608]{0:T(1024)(128)(4,1)} %bitcast.40), calls=%async_computation.2 | async-start | bytes 8388608
  75.5 2.4 %slice-start.1 = ((s8[8388608]{0:T(1024)(128)(4,1)}), s8[4194304]{0:T(1024)(128)(4,1)S(1)}, s32[]{:S(2)}) async-start(s8[8388608]{0:T(1024)(128)(4,1)} %bitcast.40), calls=%async_computation.3 | async-start | bytes 8388608
Sparse Core Ops, SparseCore 0:
  81.4 39.0 reduce-scatter.1
where the time goes:
time: 128 us; the launch traced here: 127 us
  blocking collectives  63.7 us (50%)
  waiting for transfers between devices  39.2 us (31%)
  between operations  13.4 us (10%)
  matrix products  5.98 us (5%)
  local copies, waits for them, and re-layouts  2.58 us (2%)
  other arithmetic  2.41 us (2%)
    reduce_scatter x1, waiting for transfers between devices, shards(): lax.psum_scatter(jnp.dot(attended, out_weight, preferred_element_type=jnp...  39.2 us
    all_gather x1, blocking collectives, shards(): arrived_keys = lax.all_gather(own_keys, 'cp', axis=0, tiled=True)  32.8 us
    all_gather x1, blocking collectives, shards(): arrived_values = lax.all_gather(own_values, 'cp', axis=0, tiled=True)  31 us
    dot_general x1, matrix products, shards(): jnp.dot(attended, out_weight, preferred_element_type=jnp.float32)  3.47 us
  transfers between devices with their start and end apart: 1, of which 1 were waited for; matrix products, arithmetic and copies ran while one was open for 0% of the time, Pallas kernels for 0%

commit v1 on v0

--- a/solution.py
+++ b/solution.py
@@ -17,7 +17,9 @@
     query_pos = lax.dynamic_slice_in_dim(positions, lax.axis_index("cp") * tok_rows, tok_rows, 0)
     local_queries = queries.reshape(tok_rows, head_count, HEAD)
     run_max = jnp.full((tok_rows, head_count), -1e30, jnp.float32)
-    arrived_keys = lax.all_gather(own_keys, "cp", axis=0, tiled=True)
+    arrived_keys = jnp.concatenate(
+        lax.all_to_all(jnp.stack([own_keys] * lax.axis_size("cp")), "cp", 0, 0), axis=0
+    )
     arrived_values = lax.all_gather(own_values, "cp", axis=0, tiled=True)
     allowed = (positions[None, :] <= query_pos[:, None])[:, None, :]
     scores = (

time: 128 us -> 104 us (0.81)
  blocking collectives: 63.7 us -> 34.2 us
  starting transfers between devices: 0.01 us -> 7.32 us
  waiting for transfers between devices: 39.2 us -> 36.4 us
  local copies, waits for them, and re-layouts: 2.58 us -> 4.16 us
    all_gather x1 -> x0, blocking collectives: 32.8 us -> none  [shards(): arrived_keys = lax.all_gather(own_keys, 'cp', axis=0, tiled=True)]
    all_to_all x0 -> x1, starting transfers between devices: none -> 7.28 us  [shards(): lax.all_to_all(jnp.stack([own_keys] * lax.axis_size('cp')), 'cp', 0, 0)]
    all_gather x1, blocking collectives: 31 us -> 34.2 us  [shards(): arrived_values = lax.all_gather(own_values, 'cp', axis=0, tiled=True)]
    reduce_scatter x1, waiting for transfers between devices: 39.2 us -> 36.3 us  [shards(): lax.psum_scatter(jnp.dot(attended, out_weight, preferred_element_type=jnp...]
  transfers between devices with their start and end apart: 1 -> 2, of which waited for: 1 -> 1; matrix products, arithmetic and copies ran while one was open for 0% -> 2% of each run, Pallas kernels for 0% -> 0%
where the time goes in v1:
time: 104 us
  waiting for transfers between devices  36.4 us (35%)
  blocking collectives  34.2 us (33%)
  between operations  13.5 us (13%)
  starting transfers between devices  7.32 us (7%)
  matrix products  5.98 us (6%)
  local copies, waits for them, and re-layouts  4.16 us (4%)
  other arithmetic  2.41 us (2%)
    reduce_scatter x1, waiting for transfers between devices, shards(): lax.psum_scatter(jnp.dot(attended, out_weight, preferred_element_type=jnp...  36.3 us
    all_gather x1, blocking collectives, shards(): arrived_values = lax.all_gather(own_values, 'cp', axis=0, tiled=True)  34.2 us
    all_to_all x1, starting transfers between devices, shards(): lax.all_to_all(jnp.stack([own_keys] * lax.axis_size('cp')), 'cp', 0, 0)  7.28 us
    dot_general x1, matrix products, shards(): jnp.dot(attended, out_weight, preferred_element_type=jnp.float32)  3.46 us
  transfers between devices with their start and end apart: 2, of which 1 were waited for; matrix products, arithmetic and copies ran while one was open for 2% of the time, Pallas kernels for 0%

profile of v1, /device:TPU:0, one launch (start us, length us, event | category | flops | bytes accessed | tf_op | source)
XLA Modules:
  0.0 103.9 jit_solution(4264123524561305348)
XLA Ops:
  6.5 0.0 copy-start
  6.5 0.8 constant_dynamic-slice_fusion.1
  7.4 0.8 stack.2
  8.2 7.3 %all-to-all-start = ((bf16[8,192,128]{2,1,0:T(8,128)(2,1)}), bf16[8,192,128]{2,1,0:T(8,128)(2,1)S(1)}, u32[]{:S(2)}, u32[]{:S(2)}) async-start(bf16[8,192,128]{2,1,0:T(8,128)(2,1)} %stack.2), calls=%async_computation | async-start | bytes 786432 | tf_op jit(solution)/shard_map/all_to_all | solution.py:21
  15.5 0.0 reduce-scatter.2.cloned.1.call-start
  15.5 0.8 dynamic_slice.9
  16.3 0.8 constant_dynamic-slice_fusion
  17.1 34.2 %all_gather.3 = bf16[1536,128]{1,0:T(8,128)(2,1)S(1)} all-gather(bf16[192,128]{1,0:T(8,128)(2,1)S(1)} %constant_dynamic-slice_fusion), channel_id=1, replica_groups=mesh['cp'=8,'tp'=4] {'cp'}, dimensions={0}, use_global_device_ids=true | all-gather | bytes 442368 | tf_op jit(solution)/shard_map/all_gather | solution.py:23
  51.3 0.9 broadcast_compare_fusion
  52.2 0.0 all-to-all-done
  52.2 0.0 copy-done
  52.3 1.1 %fusion = (f32[192,4]{0,1:T(4,128)S(1)}, f32[1536,192,4]{0,1,2:T(8,128)S(1)}) fusion(pred[192,1536]{1,0:T(8,128)(4,1)S(1)} %broadcast_compare_fusion, bf16[1536,128,1]{1,0,2:T(8,128)(2,1)S(1)} %bitcast.41, bf16[192,512]{1,0:T(8,128)(2,1)S(1)} %copy-done), kind=kOutput, calls=%fused_computation.3 | convolution fusion | flops 305528064 | bytes 5606400 | tf_op jit(solution)/shard_map/qhd,kd->qhk/dot_general | solution.py:26
  53.4 0.0 slice-start
  53.4 1.5 %fusion.1 = f32[192,4]{0,1:T(4,128)S(1)} fusion(f32[1536,192,4]{0,1,2:T(8,128)S(1)} %get-tuple-element.6, f32[192,4]{0,1:T(4,128)S(1)} %broadcast_maximum_fusion, pred[192,1536]{1,0:T(8,128)(4,1)S(1)} %broadcast_compare_fusion), kind=kLoop, calls=%fused_computation.4 | loop fusion | flops 5897472 | bytes 5019648 | tf_op jit(solution)/shard_map/reduce_sum | solution.py:32
  54.9 0.0 slice-start.1
  54.9 1.4 %fusion.12 = bf16[4,24,8,128]{3,2,1,0:T(8,128)(2,1)S(1)} fusion(f32[1536,192,4]{0,1,2:T(8,128)S(1)} %get-tuple-element.6, f32[192,4]{0,1:T(4,128)S(1)} %broadcast_maximum_fusion, pred[192,1536]{1,0:T(8,128)(4,1)S(1)} %broadcast_compare_fusion, bf16[1536,128]{1,0:T(8,128)(2,1)S(1)} %all_gather.3, f32[192,4]{0,1:T(4,128)S(1)} %fusion.1), kind=kOutput, calls=%fused_computation.10 | convolution fusion | flops 308084736 | bytes 5609472 | tf_op jit(solution)/shard_map/qhk,kd->qhd/dot_general | solution.py:33
  56.3 0.0 slice-done
  56.3 0.9 slice-done.1
  57.2 3.5 %convolution_convert_fusion = bf16[192,8192]{1,0:T(8,128)(2,1)} fusion(bf16[512,8192]{1,0:T(8,128)(2,1)S(1)} %bitcast.40, bf16[4,24,8,128]{3,2,1,0:T(8,128)(2,1)S(1)} %fusion.12), kind=kOutput, calls=%fused_computation | convolution fusion | flops 1612185600 | bytes 11730944 | tf_op jit(solution)/shard_map/dot_general | solution.py:45
  60.7 0.0 reduce-scatter.2.cloned.1.call-update
  60.7 36.3 %reduce-scatter.2.cloned.1.call-done = bf16[48,8192]{1,0:T(8,128)(2,1)} async-done(((bf16[192,8192]{1,0:T(8,128)(2,1)}), bf16[48,8192]{1,0:T(8,128)(2,1)}) %reduce-scatter.2.cloned.1.call-update) | async-done | bytes 786448 | tf_op jit(solution)/shard_map/reduce_scatter | solution.py:44
  (2 shorter events, 0.0 us)
Async XLA Ops:
  6.5 45.7 %copy-start = (bf16[192,512]{1,0:T(8,128)(2,1)S(1)}, bf16[192,512]{1,0:T(8,128)(2,1)}, u32[]{:S(2)}) copy-start(bf16[192,512]{1,0:T(8,128)(2,1)} %param.5) | copy-start | bytes 589828
  8.2 44.1 %all-to-all-start = ((bf16[8,192,128]{2,1,0:T(8,128)(2,1)}), bf16[8,192,128]{2,1,0:T(8,128)(2,1)S(1)}, u32[]{:S(2)}, u32[]{:S(2)}) async-start(bf16[8,192,128]{2,1,0:T(8,128)(2,1)} %stack.2), calls=%async_computation | async-start | bytes 786432 | tf_op jit(solution)/shard_map/all_to_all | solution.py:21
  15.5 81.6 %reduce-scatter.2.cloned.1.call-start = ((), (), s32[]{:S(2)}) async-start(), calls=%async_computation.2 | async-start | bytes 3932160 | tf_op jit(solution)/shard_map/reduce_scatter | solution.py:44
  53.4 2.9 %slice-start = ((s8[8388608]{0:T(1024)(128)(4,1)}), s8[4194304]{0:T(1024)(128)(4,1)S(1)}, s32[]{:S(2)}) async-start(s8[8388608]{0:T(1024)(128)(4,1)} %bitcast.39), calls=%async_computation.3 | async-start | bytes 8388608
  54.9 2.4 %slice-start.1 = ((s8[8388608]{0:T(1024)(128)(4,1)}), s8[4194304]{0:T(1024)(128)(4,1)S(1)}, s32[]{:S(2)}) async-start(s8[8388608]{0:T(1024)(128)(4,1)} %bitcast.39), calls=%async_computation.4 | async-start | bytes 8388608
Sparse Core Ops, SparseCore 0:
  60.8 36.1 reduce-scatter.1
